TPU v7x, 32 devices: a whole 2x2x4 slice. The times are simulated.
32 devices in a mesh: batch: 4 (over z), seq: 8 (over y, x, core).
Axes of the slice: x: 2, y: 2, z: 4, core: 2. Of those that a mesh axis runs over, the one named last changes fastest.
Arguments:
- tokens: bfloat16 [10240, 8192], P(('batch', 'seq')), may hold values from -6 to 6
- out_grad: bfloat16 [10240, 8192], P(('batch', 'seq')), may hold values from -0.109375 to 0.109375
- gate_pre: bfloat16 [10240, 768], P(('batch', 'seq')), may hold values from -8 to 8
- up_pre: bfloat16 [10240, 768], P(('batch', 'seq')), may hold values from -6 to 6
- hidden_grad: bfloat16 [10240, 768], P(('batch', 'seq')), may hold values from -0.0625 to 0.0625
Outputs:
- gate_weight_grad: float32 [8192, 768], P(('seq', 'batch'))
- up_weight_grad: float32 [8192, 768], P(('seq', 'batch'))
- down_weight_grad: float32 [8192, 768], P(('seq', 'batch'))
All inputs are finite; a program needn't handle non-finite values.
Results may differ from a plain program's by a relative error of at most 0.019.
Values may be sent and summed in bfloat16 or wider, within the bound.
A program may use at most 192 MiB of HBM per device.

v0:
```python
import functools

import jax
import jax.numpy as jnp
from jax import lax
from jax.experimental import pallas as pl
from jax.experimental.pallas import tpu as pltpu
from jax.sharding import PartitionSpec as P

MESH = pl.DeviceIdType.MESH
LANES = 128


def bit_count(n):
    return n.bit_length() - 1


def flip(value, mask):
    out, bit = value, 1
    while bit <= mask:
        if mask & bit:
            out = out + bit * (1 - 2 * ((value // bit) % 2))
        bit *= 2
    return out


class Plan:
    def __init__(self, n_batch, n_seq, tok, width, hidden):
        self.n_batch, self.n_seq, self.tok, self.width, self.hidden = n_batch, n_seq, tok, width, hidden
        self.chips = n_seq // 2
        self.seq_bits, self.batch_bits = bit_count(self.chips), bit_count(n_batch)
        self.rows = width // (n_batch * n_seq)
        self.group = max(1, LANES // self.rows)
        self.block = self.group * self.rows
        self.n_groups = n_batch // self.group
        total = 3 * hidden
        units = total // LANES
        late = max(2, units // 6)
        early = (units - late) // 2
        cuts = [0, early, units - late, units - late // 2, units]
        self.spans = [(a * LANES, b * LANES) for a, b in zip(cuts[:-1], cuts[1:])]
        self.ascending = [True, False, True, False]
        self.batch_first = [False, False, True, True]

    def seq_bit(self, cls, stage):
        return stage if self.ascending[cls] else self.seq_bits - 1 - stage

    def position(self, cls, u):
        if not self.ascending[cls]:
            return u
        return sum(((u // (1 << i)) % 2) * (1 << (self.seq_bits - 1 - i)) for i in range(self.seq_bits))

    def pieces(self, lo, hi, step):
        out = []
        while lo < hi:
            end = min(hi, (lo // step + 1) * step)
            out.append((lo, end))
            lo = end
        return out


def low_bit(m):
    return (m & -m).bit_length() - 1


def kernel(plan, tokens, out_grad, gate_pre, up_pre, hidden_grad, out_gate, out_up, out_down, *scratch):
    p = plan
    T, R, M, C, NB = p.tok, p.rows, p.block, p.chips, p.n_batch
    n_cls, sb, bb = len(p.spans), p.seq_bits, p.batch_bits
    scratch = list(scratch)
    raw, hid, tok_v, grad_v = (scratch.pop(0) for _ in range(4))
    terms = [scratch.pop(0) for _ in range(n_cls)]
    seq_in = [[scratch.pop(0) for _ in range(sb)] for _ in range(n_cls)]
    batch_in = [[scratch.pop(0) for _ in range(bb)] for _ in range(n_cls)]
    raw_sem, load_sem, swap_sem, swap_out, seq_send, seq_recv, batch_send, batch_recv = scratch
    outs = (out_gate, out_up, out_down)

    b_me, s_me = lax.axis_index("batch"), lax.axis_index("seq")
    core, chip = s_me % 2, s_me // 2
    twin = (b_me, s_me + 1 - 2 * core)
    seq_peer = [(b_me, flip(s_me, 2 << i)) for i in range(sb)]
    batch_peer = [(flip(b_me, 1 << i), s_me) for i in range(bb)]

    pre = (gate_pre, up_pre, hidden_grad)
    for i, ref in enumerate(pre):
        pltpu.make_async_copy(ref, raw.at[i, pl.ds(0, T)], raw_sem.at[0]).start()

    def column(g, u, side):
        k = flip(chip, u)
        first = flip(b_me // p.group, g) * p.group
        return pl.multiple_of(((k * 2 + side) * NB + first) * R, M)

    sends = []
    groups = list(range(p.n_groups - 1, -1, -1))

    def load(g):
        for a, (src, dst) in enumerate(((tokens, tok_v), (out_grad, grad_v))):
            for u in range(C):
                pltpu.make_async_copy(
                    src.at[:, pl.ds(column(g, u, core), M)], dst.at[g, u, pl.ds(0, T)], load_sem.at[g, a]
                ).start()

    def swap(g):
        for a, (src, dst) in enumerate(((tokens, tok_v), (out_grad, grad_v))):
            for u in range(C):
                pltpu.make_async_remote_copy(
                    src_ref=src.at[:, pl.ds(column(g, u, 1 - core), M)],
                    dst_ref=dst.at[g, u, pl.ds(T, T)],
                    send_sem=swap_out.at[g, a],
                    recv_sem=swap_sem.at[g, a],
                    device_id=twin,
                    device_id_type=MESH,
                ).start()

    for g in groups:
        load(g)

    barrier = pltpu.get_barrier_semaphore()
    peers = [twin] + seq_peer + batch_peer
    for peer in peers:
        pl.semaphore_signal(barrier, inc=1, device_id=peer, device_id_type=MESH)
    pl.semaphore_wait(barrier, len(peers))

    for i, ref in enumerate(pre):
        pltpu.make_async_remote_copy(
            src_ref=ref, dst_ref=raw.at[i, pl.ds(T, T)], send_sem=raw_sem.at[1], recv_sem=raw_sem.at[2],
            device_id=twin, device_id_type=MESH,
        ).start()
    for g in groups:
        swap(g)

    def activate(side):
        step = 32
        def body(i, carry):
            at = pl.ds(pl.multiple_of(side * T + i * step, step), step)
            gate_val = raw[0, at, :].astype(jnp.float32)
            up_val = raw[1, at, :].astype(jnp.float32)
            grad_val = raw[2, at, :].astype(jnp.float32)
            sig = jax.nn.sigmoid(gate_val)
            act = gate_val * sig
            F = p.hidden
            hid[at, 0:F] = (grad_val * up_val * sig * (1.0 + gate_val * (1.0 - sig))).astype(jnp.bfloat16)
            hid[at, F:2 * F] = (grad_val * act).astype(jnp.bfloat16)
            hid[at, 2 * F:3 * F] = (act * up_val).astype(jnp.bfloat16)
            return carry
        lax.fori_loop(0, T // step, body, 0)

    def wait_bytes(ref, sem):
        pltpu.make_async_copy(ref, ref, sem).wait()

    wait_bytes(raw.at[:, pl.ds(0, T)], raw_sem.at[0])
    activate(0)
    wait_bytes(raw.at[:, pl.ds(T, T)], raw_sem.at[2])
    activate(1)

    def arrive(g):
        for a, dst in enumerate((tok_v, grad_v)):
            wait_bytes(dst.at[g, :, pl.ds(0, T)], load_sem.at[g, a])
            wait_bytes(dst.at[g, :, pl.ds(T, T)], swap_sem.at[g, a])

    def compute_block(g, u):
        feats, grads = tok_v[g, u], grad_v[g, u]
        for cls, (lo, hi) in enumerate(p.spans):
            pos = p.position(cls, u)
            for a, b in p.pieces(lo, hi, 2 * p.hidden):
                value = lax.dot_general(
                    feats if a < 2 * p.hidden else grads, hid[:, a:b],
                    (((0,), (0,)), ((), ())), preferred_element_type=jnp.float32,
                ).astype(jnp.bfloat16)
                for h in range(p.group):
                    m = g if p.group == 1 else g * p.group + flip(b_me % p.group, h)
                    terms[cls][m, pos, :, a - lo:b - lo] = value[h * R:(h + 1) * R]

    def compute(g):
        arrive(g)

        def body(u, carry):
            compute_block(g, u)
            return carry
        lax.fori_loop(0, C, body, 0)

    step = min(R, 32)

    def gather(cls, m, first, count, extra):
        def body(i, carry):
            blk, at = first + i // (R // step), pl.ds(pl.multiple_of((i % (R // step)) * step, step), step)
            value = terms[cls][m, blk, at, :].astype(jnp.float32)
            for ref, slot in extra:
                value = value + ref[slot, blk, at, :].astype(jnp.float32)
            terms[cls][m, blk, at, :] = value.astype(jnp.bfloat16)
            return carry
        if extra:
            lax.fori_loop(0, count * (R // step), body, 0)

    def finish(cls, extra):
        lo, hi = p.spans[cls]
        def body(i, carry):
            at = pl.ds(pl.multiple_of(i * step, step), step)
            for a, b in p.pieces(lo, hi, p.hidden):
                value = terms[cls][0, 0, at, a - lo:b - lo].astype(jnp.float32)
                for ref, slot in extra:
                    value = value + ref[slot, 0, at, a - lo:b - lo].astype(jnp.float32)
                base = (a // p.hidden) * p.hidden
                outs[a // p.hidden][at, a - base:b - base] = value
            return carry
        lax.fori_loop(0, R // step, body, 0)

    def seq_slot(cls, m):
        return 0 if p.batch_first[cls] else m

    def halves(stage):
        return 2 if C >> (stage + 1) > 1 else 1

    def seq_copy(cls, m, stage, part):
        count = C >> (stage + 1)
        size = count // halves(stage)
        first = count - size if part == 0 else 0
        slot = seq_slot(cls, m)
        return pltpu.make_async_remote_copy(
            src_ref=terms[cls].at[m, pl.ds(count + first, size)],
            dst_ref=seq_in[cls][stage].at[slot, pl.ds(first, size)],
            send_sem=seq_send.at[cls, 2 * stage + part, slot],
            recv_sem=seq_recv.at[cls, 2 * stage + part, slot],
            device_id=seq_peer[p.seq_bit(cls, stage)],
            device_id_type=MESH,
        )

    def batch_copy(cls, m):
        stage = low_bit(m)
        slot = m >> (stage + 1)
        count = C if p.batch_first[cls] else 1
        return pltpu.make_async_remote_copy(
            src_ref=terms[cls].at[m, pl.ds(0, count)],
            dst_ref=batch_in[cls][stage].at[slot],
            send_sem=batch_send.at[cls, stage, slot],
            recv_sem=batch_recv.at[cls, stage, slot],
            device_id=batch_peer[stage],
            device_id_type=MESH,
        )

    def start(copy):
        copy.start()
        sends.append(copy)

    def from_seq(cls, m, stages):
        return [(seq_in[cls][j], seq_slot(cls, m)) for j in range(stages)]

    def from_batch(cls, m):
        count = bb if m == 0 else low_bit(m)
        return [(batch_in[cls][j], m >> (j + 1)) for j in range(count)]

    def wait_batch(cls, m):
        count = bb if m == 0 else low_bit(m)
        for j in range(count):
            batch_copy(cls, m + (1 << j)).wait_recv()

    def wait_seq(cls, m, stage):
        if stage >= 0:
            seq_copy(cls, m, stage, 0).wait_recv()
        if stage >= 1:
            seq_copy(cls, m, stage - 1, 1).wait_recv()

    def seq_stage(cls, m, stage, base, parts=(0, 1)):
        wait_seq(cls, m, stage - 1)
        count = C >> (stage + 1)
        gather(cls, m, count, count, base + from_seq(cls, m, stage))
        for part in parts[:halves(stage)]:
            start(seq_copy(cls, m, stage, part))

    def batch_last(cls, m):
        wait_seq(cls, m, sb - 1)
        wait_batch(cls, m)
        extra = from_seq(cls, m, sb) + from_batch(cls, m)
        if m == 0:
            finish(cls, extra)
        else:
            gather(cls, m, 0, 1, extra)
            start(batch_copy(cls, m))

    def batch_early(cls, m):
        wait_batch(cls, m)
        if m:
            gather(cls, m, 0, C, from_batch(cls, m))
            start(batch_copy(cls, m))
        else:
            seq_stage(cls, 0, 0, from_batch(cls, 0))

    plain = [c for c in range(n_cls) if not p.batch_first[c]]
    early = [c for c in range(n_cls) if p.batch_first[c]]
    order = list(range(NB - 1, -1, -1))
    done = set()

    def need(i):
        if i < NB and order[i] // p.group not in done:
            done.add(order[i] // p.group)
            compute(order[i] // p.group)

    def first_round():
        g = groups[0]
        done.add(g)
        arrive(g)
        upper = [u for u in range(C) if any(p.position(c, u) >= C - C // 4 for c in plain)] if p.group == 1 else []
        for u in upper:
            compute_block(g, u)
        split = bool(upper) and halves(0) == 2
        if split:
            for cls in plain:
                start(seq_copy(cls, order[0], 0, 0))
        rest = [u for u in range(C) if u not in upper]
        if rest == list(range(len(rest))):
            def body(u, carry):
                compute_block(g, u)
                return carry
            lax.fori_loop(0, len(rest), body, 0)
        else:
            for u in rest:
                compute_block(g, u)
        for cls in plain:
            for part in range(1 if split else 0, halves(0)):
                start(seq_copy(cls, order[0], 0, part))
        if order[0] % 2:
            for cls in early:
                batch_early(cls, order[0])

    first_round()
    for i in range(1, NB + 1):
        before = order[i - 1]
        need(i)
        if i == 1:
            need(2)
        for stage in range(1, sb):
            for cls in plain:
                seq_stage(cls, before, stage, [])
        if i < NB:
            for cls in plain:
                seq_stage(cls, order[i], 0, [])
        if i + 1 < NB:
            need(i + 1)
        for cls in early:
            if i + 1 < NB and order[i + 1] % 2:
                batch_early(cls, order[i + 1])
            if i < NB and order[i] and order[i] % 2 == 0:
                batch_early(cls, order[i])
        if i == NB:
            for cls in early:
                batch_early(cls, 0)
        for cls in plain:
            batch_last(cls, before)
    for stage in range(1, sb):
        for cls in early:
            seq_stage(cls, 0, stage, from_batch(cls, 0))
    for cls in early:
        wait_seq(cls, 0, sb - 1)
        finish(cls, from_batch(cls, 0) + from_seq(cls, 0, sb))

    for copy in sends:
        copy.wait_send()
    wait_bytes(raw.at[:, pl.ds(T, T)], raw_sem.at[1])
    for g in groups:
        for a, dst in enumerate((tok_v, grad_v)):
            wait_bytes(dst.at[g, :, pl.ds(T, T)], swap_out.at[g, a])


def on_device(n_batch, n_seq, tokens, out_grad, gate_pre, up_pre, hidden_grad):
    tok, width = tokens.shape
    hidden = gate_pre.shape[1]
    p = Plan(n_batch, n_seq, tok, width, hidden)
    C, R, bf16 = p.chips, p.rows, jnp.bfloat16
    scratch = [
        pltpu.VMEM((3, 2 * tok, hidden), bf16),
        pltpu.VMEM((2 * tok, 3 * hidden), bf16),
        pltpu.VMEM((p.n_groups, C, 2 * tok, p.block), bf16),
        pltpu.VMEM((p.n_groups, C, 2 * tok, p.block), bf16),
    ]
    sizes = [hi - lo for lo, hi in p.spans]
    scratch += [pltpu.VMEM((n_batch, C, R, size), bf16) for size in sizes]
    for cls, size in enumerate(sizes):
        slots = 1 if p.batch_first[cls] else n_batch
        scratch += [pltpu.VMEM((slots, C >> (j + 1), R, size), bf16) for j in range(p.seq_bits)]
    for cls, size in enumerate(sizes):
        blocks = C if p.batch_first[cls] else 1
        scratch += [pltpu.VMEM((n_batch >> (j + 1), blocks, R, size), bf16) for j in range(p.batch_bits)]
    n_cls = len(sizes)
    dma = pltpu.SemaphoreType.DMA
    scratch += [
        dma((3,)),
        dma((p.n_groups, 2)), dma((p.n_groups, 2)), dma((p.n_groups, 2)),
        dma((n_cls, 2 * p.seq_bits, n_batch)), dma((n_cls, 2 * p.seq_bits, n_batch)),
        dma((n_cls, p.batch_bits, n_batch // 2)), dma((n_cls, p.batch_bits, n_batch // 2)),
    ]
    out = jax.ShapeDtypeStruct((R, hidden), jnp.float32)
    return pl.pallas_call(
        functools.partial(kernel, p),
        out_shape=(out, out, out),
        in_specs=[pl.BlockSpec(memory_space=pltpu.HBM)] * 5,
        out_specs=[pl.BlockSpec(memory_space=pltpu.VMEM)] * 3,
        scratch_shapes=scratch,
        compiler_params=pltpu.CompilerParams(
            collective_id=0, has_side_effects=True, vmem_limit_bytes=67043328
        ),
    )(tokens, out_grad, gate_pre, up_pre, hidden_grad)


def solution(mesh):
    rows = P(("batch", "seq"), None)
    outs = P(("seq", "batch"), None)
    body = functools.partial(on_device, mesh.shape["batch"], mesh.shape["seq"])
    return jax.shard_map(
        body, mesh=mesh, in_specs=(rows,) * 5, out_specs=(outs,) * 3, check_vma=False
    )
```

profile of v0, /device:TPU:0, one launch (start us, length us, event | category | flops | bytes accessed | tf_op | source)
XLA Modules:
  0.0 160.9 jit_solution(7529635703165798772)
XLA Ops:
  0.6 154.0 %shard_map.76 = (f32[256,768]{1,0:T(8,128)}, f32[256,768]{1,0:T(8,128)}, f32[256,768]{1,0:T(8,128)}) custom-call(bf16[320,8192]{1,0:T(8,128)(2,1)} %tokens.1, bf16[320,8192]{1,0:T(8,128)(2,1)} %out_grad.1, bf16[320,768]{1,0:T(8,128)(2,1)} %gate_pre.1, bf16[320,768]{1,0:T(8,128)(2,1)} %up_pre.1, bf16[320,768]{1,0:T(8,128)(2,1)} %hidden_grad.1), custom_call_target="tpu_custom_call" | custom-call | tf_op jit(solution)/shard_map/pallas_call | solution.py:392
  154.7 2.1 %copy.11 = f32[256,768]{1,0:T(8,128)} copy(f32[256,768]{1,0:T(8,128)} %get-tuple-element.6) | data formatting | bytes 1572864
  156.7 2.1 %copy.12 = f32[256,768]{1,0:T(8,128)} copy(f32[256,768]{1,0:T(8,128)} %get-tuple-element.7) | data formatting | bytes 1572864
  158.8 2.1 %copy.13 = f32[256,768]{1,0:T(8,128)} copy(f32[256,768]{1,0:T(8,128)} %get-tuple-element.8) | data formatting | bytes 1572864
where the time goes:
time: 161 us
  Pallas kernels  154 us (96%)
  local copies, waits for them, and re-layouts  6.19 us (4%)
    pallas_call x1, Pallas kernels, on_device(): pl.pallas_call(functools.partial(kernel, p), out_shape=(out, out, out), i...  154 us
    unnamed x3, local copies, waits for them, and re-layouts  6.19 us

commit v1 on v0

--- a/solution.py
+++ b/solution.py
@@ -361,10 +361,291 @@
             wait_bytes(dst.at[g, :, pl.ds(T, T)], swap_out.at[g, a])
 
 
+X, Y, Z0, Z1 = range(4)
+
+
+class Flow:
+    def __init__(self, source, order, rows, cols, out, out_col):
+        self.source, self.order, self.rows, self.cols = source, order, rows, cols
+        self.out, self.out_col = out, out_col
+        self.n = len(order)
+        self.shape = (1 << self.n, rows[1] - rows[0], cols[1] - cols[0])
+
+    def dense(self, block):
+        return sum(((block >> b) & 1) << (self.n - 1 - i) for i, b in enumerate(self.order))
+
+    def block(self, d):
+        return sum(((d >> (self.n - 1 - i)) & 1) << b for i, b in enumerate(self.order))
+
+    def stage(self, d):
+        return self.n - d.bit_length()
+
+    def incoming(self, d):
+        return [d + (1 << (self.n - 1 - i)) for i in range(self.stage(d))]
+
+
+class Exchange:
+    def __init__(self, n_batch, n_seq, tok, width, hidden):
+        self.n_batch, self.n_seq, self.tok, self.width, self.hidden = n_batch, n_seq, tok, width, hidden
+        self.rows = R = width // (n_batch * n_seq)
+        unit, half = hidden // 6, R // 2
+        full = (0, R)
+        batch_first, y_first, x_first = (Z0, Z1, X, Y), (Y, X, Z0, Z1), (X, Y, Z0, Z1)
+        def down(order, rows, a, b):
+            return Flow("down", order, rows, (a * unit, b * unit), 2, 0)
+        self.flows = [
+            Flow("up", (Y, Z0, Z1), full, (0, hidden), 0, 0),
+            Flow("up", (Y, Z0, Z1), full, (hidden, 2 * hidden), 1, hidden),
+            down(batch_first, full, 0, 2),
+            down(batch_first, (0, half), 2, 3),
+            down(x_first, (half, R), 2, 3),
+            down(y_first, full, 3, 6),
+        ]
+
+    @staticmethod
+    def fits(n_batch, n_seq, tok, width, hidden):
+        return n_batch == 4 and n_seq == 8 and hidden % (6 * LANES) == 0 and width % (n_batch * n_seq * LANES) == 0
+
+    def tasks(self):
+        out = [("tok", k, m) for k in (1, 0) for m in (3, 1, 2, 0)]
+        out += [("forward",)]
+        out += [("down", u, m) for u in range(4) for m in range(4)]
+        out += [("up", k, m) for k in range(2) for m in range(4)]
+        out += [("advance", c, d) for c, f in enumerate(self.flows) for d in range(1 << f.n)]
+        return out
+
+
+ORDER = (
+    18, 107, 58, 22, 21, 60, 9, 14, 20, 109, 16, 10, 15, 63, 19, 24,
+    17, 12, 11, 23, 112, 62, 13, 64, 108, 61, 111, 55, 54, 110, 56, 104,
+    105, 59, 4, 57, 106, 8, 53, 32, 40, 102, 100, 79, 2, 78, 73, 75,
+    80, 28, 48, 74, 77, 76, 1, 98, 70, 71, 36, 31, 38, 6, 44, 46,
+    30, 94, 5, 72, 27, 39, 34, 96, 103, 92, 52, 26, 95, 88, 42, 3,
+    47, 51, 35, 87, 50, 90, 93, 101, 86, 29, 37, 89, 84, 91, 99, 7,
+    49, 43, 45, 68, 67, 97, 82, 85, 83, 69, 25, 66, 33, 41, 81, 65,
+)
+
+
+def exchange_kernel(plan, tokens, out_grad, gate_pre, up_pre, hidden_grad, out_gate, out_up, out_down, *scratch):
+    p = plan
+    T, R, F, NB = p.tok, p.rows, p.hidden, p.n_batch
+    n_flows = len(p.flows)
+    scratch = list(scratch)
+    raw, hid, cot, tok_v, grad_v = (scratch.pop(0) for _ in range(5))
+    own = [scratch.pop(0) for _ in range(n_flows)]
+    got = [scratch.pop(0) for _ in range(n_flows)]
+    raw_sem, cot_sem, load_g, swap_g, sent_g, load_t, swap_t, sent_t, send_x, recv_x, flow_send, flow_recv = scratch
+    outs = (out_gate, out_up, out_down)
+
+    b_me, s_me = lax.axis_index("batch"), lax.axis_index("seq")
+    core, chip = s_me % 2, s_me // 2
+
+    def device(block, other=0):
+        return (flip(b_me, block >> 2), flip(s_me, 2 * (block & 3) + other))
+
+    def columns(block, other=0):
+        b, s = device(block, other)
+        return pl.ds(pl.multiple_of((s * NB + b) * R, R), R)
+
+    twin, across, crossed = device(0, 1), device(1 << X), device(1 << X, 1)
+    peer = [device(1 << bit) for bit in range(4)]
+    sends = []
+
+    def remote(src, dst, send_sem, recv_sem, to):
+        return pltpu.make_async_remote_copy(
+            src_ref=src, dst_ref=dst, send_sem=send_sem, recv_sem=recv_sem, device_id=to, device_id_type=MESH
+        )
+
+    def start(copy):
+        copy.start()
+        sends.append(copy)
+
+    def raw_copies():
+        return [pltpu.make_async_copy(ref, raw.at[i, pl.ds(0, T)], raw_sem.at[0, i])
+                for i, ref in enumerate((gate_pre, up_pre, hidden_grad))]
+
+    def raw_swaps():
+        return [remote(ref, raw.at[i, pl.ds(T, T)], raw_sem.at[1, i], raw_sem.at[2, i], twin)
+                for i, ref in enumerate((gate_pre, up_pre, hidden_grad))]
+
+    def grad_copy(u, m):
+        return pltpu.make_async_copy(
+            out_grad.at[:, columns(u + 4 * m)], grad_v.at[u, m, pl.ds(0, T)], load_g.at[u, m])
+
+    def grad_swap(u, m):
+        return remote(out_grad.at[:, columns(u + 4 * m, 1)], grad_v.at[u, m, pl.ds(T, T)],
+                      sent_g.at[u, m], swap_g.at[u, m], twin)
+
+    def tok_copy(k, m):
+        return pltpu.make_async_copy(
+            tokens.at[:, columns(2 * k + 4 * m)], tok_v.at[k, m, pl.ds(0, T)], load_t.at[k, m])
+
+    def tok_swap(k, m):
+        return remote(tokens.at[:, columns(2 * k + 4 * m, 1)], tok_v.at[k, m, pl.ds(T, T)],
+                      sent_t.at[k, m], swap_t.at[k, m], twin)
+
+    def tok_sends(k, m):
+        return [remote(tokens.at[:, columns(1 + 2 * k + 4 * m, c)], tok_v.at[k, m, pl.ds((2 + c) * T, T)],
+                       send_x.at[k, m, c], recv_x.at[k, m, c], to) for c, to in enumerate((across, crossed))]
+
+    def cot_send():
+        return remote(cot.at[pl.ds(0, T)], cot.at[pl.ds(2 * T, T)], cot_sem.at[0], cot_sem.at[1], across)
+
+    def cot_forward():
+        return remote(cot.at[pl.ds(2 * T, T)], cot.at[pl.ds(3 * T, T)], cot_sem.at[2], cot_sem.at[3], twin)
+
+    def flow_copy(c, d):
+        f = p.flows[c]
+        return remote(own[c].at[d], got[c].at[d], flow_send.at[c, d], flow_recv.at[c, d], peer[f.order[f.stage(d)]])
+
+    def activate(side):
+        step = 32
+        def body(i, carry):
+            at = pl.ds(pl.multiple_of(side * T + i * step, step), step)
+            gate_val = raw[0, at, :].astype(jnp.float32)
+            up_val = raw[1, at, :].astype(jnp.float32)
+            grad_val = raw[2, at, :].astype(jnp.float32)
+            sig = jax.nn.sigmoid(gate_val)
+            act = gate_val * sig
+            cot[at, 0:F] = (grad_val * up_val * sig * (1.0 + gate_val * (1.0 - sig))).astype(jnp.bfloat16)
+            cot[at, F:2 * F] = (grad_val * act).astype(jnp.bfloat16)
+            hid[at, :] = (act * up_val).astype(jnp.bfloat16)
+            return carry
+        lax.fori_loop(0, T // step, body, 0)
+
+    dot = functools.partial(
+        lax.dot_general, dimension_numbers=(((0,), (0,)), ((), ())), preferred_element_type=jnp.float32)
+
+    def keep(source, block, value):
+        for c, f in enumerate(p.flows):
+            if f.source == source:
+                own[c][f.dense(block)] = value[f.rows[0]:f.rows[1], f.cols[0]:f.cols[1]].astype(jnp.bfloat16)
+
+    def down(u, m):
+        grad_copy(u, m).wait()
+        grad_swap(u, m).wait_recv()
+        keep("down", u + 4 * m, dot(grad_v[u, m], hid[...]))
+
+    cot_left = [True]
+
+    def up(k, m):
+        if cot_left:
+            cot_left.pop()
+            cot_forward().wait_recv()
+        tok_copy(k, m).wait()
+        tok_swap(k, m).wait_recv()
+        for copy in tok_sends(k, m):
+            copy.wait_recv()
+        keep("up", 2 * k + 4 * m, dot(tok_v[k, m], cot[...]))
+
+    def tok(k, m):
+        for copy in tok_sends(k, m):
+            start(copy)
+
+    def forward():
+        cot_send().wait_recv()
+        start(cot_forward())
+
+    def advance(c, d):
+        f = p.flows[c]
+        entries = f.incoming(d)
+        for e in entries:
+            flow_copy(c, e).wait_recv()
+        rows = f.shape[1]
+        step = 32
+
+        def body(i, carry):
+            at = pl.ds(pl.multiple_of(i * step, step), step)
+            value = own[c][d, at, :].astype(jnp.float32)
+            for e in entries:
+                value = value + got[c][e, at, :].astype(jnp.float32)
+            if d:
+                own[c][d, at, :] = value.astype(jnp.bfloat16)
+            else:
+                to = pl.ds(pl.multiple_of(f.rows[0] + i * step, step), step)
+                outs[f.out][to, f.cols[0] - f.out_col:f.cols[1] - f.out_col] = value
+            return carry
+        if entries:
+            lax.fori_loop(0, rows // step, body, 0)
+        if d:
+            start(flow_copy(c, d))
+
+    tasks = p.tasks()
+    order = [tasks[i] for i in ORDER]
+    downs = [t[1:] for t in order if t[0] == "down"]
+    ups = [t[1:] for t in order if t[0] == "up"]
+
+    for copy in raw_copies():
+        copy.start()
+    for u, m in downs:
+        grad_copy(u, m).start()
+    for k, m in ups:
+        tok_copy(k, m).start()
+
+    barrier = pltpu.get_barrier_semaphore()
+    peers = [twin, crossed] + peer
+    for to in peers:
+        pl.semaphore_signal(barrier, inc=1, device_id=to, device_id_type=MESH)
+    pl.semaphore_wait(barrier, len(peers))
+
+    for copy in raw_swaps():
+        start(copy)
+    tok(1, 3)
+    for u, m in downs:
+        start(grad_swap(u, m))
+    for copy in raw_copies():
+        copy.wait()
+    activate(0)
+    start(cot_send())
+    for k, m in ups:
+        start(tok_swap(k, m))
+    for copy in raw_swaps():
+        copy.wait_recv()
+    activate(1)
+
+    run = {"tok": tok, "forward": forward, "down": down, "up": up, "advance": advance}
+    for task in order:
+        run[task[0]](*task[1:])
+
+    for copy in sends:
+        copy.wait_send()
+
+
+def exchange_on_device(p, *args):
+    T, R, F, bf16 = p.tok, p.rows, p.hidden, jnp.bfloat16
+    scratch = [
+        pltpu.VMEM((3, 2 * T, F), bf16),
+        pltpu.VMEM((2 * T, F), bf16),
+        pltpu.VMEM((4 * T, 2 * F), bf16),
+        pltpu.VMEM((2, 4, 4 * T, R), bf16),
+        pltpu.VMEM((4, 4, 2 * T, R), bf16),
+    ]
+    scratch += [pltpu.VMEM(f.shape, bf16) for f in p.flows] * 2
+    dma, n_flows = pltpu.SemaphoreType.DMA, len(p.flows)
+    scratch += [dma((3, 3)), dma((4,))] + [dma((4, 4))] * 3 + [dma((2, 4))] * 3
+    scratch += [dma((2, 4, 2))] * 2 + [dma((n_flows, 16))] * 2
+    out = jax.ShapeDtypeStruct((R, F), jnp.float32)
+    return pl.pallas_call(
+        functools.partial(exchange_kernel, p),
+        out_shape=(out, out, out),
+        in_specs=[pl.BlockSpec(memory_space=pltpu.HBM)] * 5,
+        out_specs=[pl.BlockSpec(memory_space=pltpu.VMEM)] * 3,
+        scratch_shapes=scratch,
+        compiler_params=pltpu.CompilerParams(
+            collective_id=0, has_side_effects=True, vmem_limit_bytes=67043328
+        ),
+    )(*args)
+
+
 def on_device(n_batch, n_seq, tokens, out_grad, gate_pre, up_pre, hidden_grad):
     tok, width = tokens.shape
     hidden = gate_pre.shape[1]
-    p = Plan(n_batch, n_seq, tok, width, hidden)
+    sizes = (n_batch, n_seq, tok, width, hidden)
+    if Exchange.fits(*sizes):
+        return exchange_on_device(
+            Exchange(*sizes), tokens, out_grad, gate_pre, up_pre, hidden_grad
+        )
+    p = Plan(*sizes)
     C, R, bf16 = p.chips, p.rows, jnp.bfloat16
     scratch = [
         pltpu.VMEM((3, 2 * tok, hidden), bf16),

time: 161 us -> 138 us (0.86)
  Pallas kernels: 154 us -> 131 us
    pallas_call x1, Pallas kernels: 154 us -> 131 us  [exchange_on_device(): pl.pallas_call(functools.partial(exchange_kernel, p), out_shape=(out, out...]
where the time goes in v1:
time: 138 us
  Pallas kernels  131 us (95%)
  local copies, waits for them, and re-layouts  6.19 us (4%)
    pallas_call x1, Pallas kernels, exchange_on_device(): pl.pallas_call(functools.partial(exchange_kernel, p), out_shape=(out, out...  131 us
    unnamed x3, local copies, waits for them, and re-layouts  6.19 us

profile of v1, /device:TPU:0, one launch (start us, length us, event | category | flops | bytes accessed | tf_op | source)
XLA Modules:
  0.0 137.6 jit_solution(10780122712068296320)
XLA Ops:
  0.6 130.8 %shard_map.76 = (f32[256,768]{1,0:T(8,128)}, f32[256,768]{1,0:T(8,128)}, f32[256,768]{1,0:T(8,128)}) custom-call(bf16[320,8192]{1,0:T(8,128)(2,1)} %tokens.1, bf16[320,8192]{1,0:T(8,128)(2,1)} %out_grad.1, bf16[320,768]{1,0:T(8,128)(2,1)} %gate_pre.1, bf16[320,768]{1,0:T(8,128)(2,1)} %up_pre.1, bf16[320,768]{1,0:T(8,128)(2,1)} %hidden_grad.1), custom_call_target="tpu_custom_call" | custom-call | tf_op jit(solution)/shard_map/pallas_call | solution.py:628
  131.4 2.1 %copy.11 = f32[256,768]{1,0:T(8,128)} copy(f32[256,768]{1,0:T(8,128)} %get-tuple-element.6) | data formatting | bytes 1572864
  133.5 2.1 %copy.12 = f32[256,768]{1,0:T(8,128)} copy(f32[256,768]{1,0:T(8,128)} %get-tuple-element.7) | data formatting | bytes 1572864
  135.5 2.1 %copy.13 = f32[256,768]{1,0:T(8,128)} copy(f32[256,768]{1,0:T(8,128)} %get-tuple-element.8) | data formatting | bytes 1572864

commit v2 on v1

--- a/solution.py
+++ b/solution.py
@@ -1,4 +1,5 @@
 import functools
+import math
 
 import jax
 import jax.numpy as jnp
@@ -415,26 +416,28 @@
         return out
 
 
+SPARE = 6 << 20
 ORDER = (
-    18, 107, 58, 22, 21, 60, 9, 14, 20, 109, 16, 10, 15, 63, 19, 24,
-    17, 12, 11, 23, 112, 62, 13, 64, 108, 61, 111, 55, 54, 110, 56, 104,
-    105, 59, 4, 57, 106, 8, 53, 32, 40, 102, 100, 79, 2, 78, 73, 75,
-    80, 28, 48, 74, 77, 76, 1, 98, 70, 71, 36, 31, 38, 6, 44, 46,
-    30, 94, 5, 72, 27, 39, 34, 96, 103, 92, 52, 26, 95, 88, 42, 3,
-    47, 51, 35, 87, 50, 90, 93, 101, 86, 29, 37, 89, 84, 91, 99, 7,
-    49, 43, 45, 68, 67, 97, 82, 85, 83, 69, 25, 66, 33, 41, 81, 65,
+    22, 111, 60, 14, 15, 59, 24, 23, 19, 112, 13, 10, 16, 79, 20, 78,
+    12, 17, 57, 9, 21, 108, 11, 18, 74, 73, 80, 61, 71, 107, 70, 64,
+    109, 72, 76, 62, 53, 106, 8, 56, 105, 104, 58, 54, 110, 4, 32, 48,
+    75, 63, 2, 100, 40, 77, 28, 55, 1, 44, 69, 31, 6, 46, 36, 30,
+    5, 47, 27, 42, 3, 38, 26, 94, 102, 43, 39, 7, 29, 34, 89, 86,
+    96, 45, 92, 67, 90, 101, 25, 35, 103, 88, 37, 93, 98, 68, 91, 95,
+    52, 41, 51, 84, 99, 85, 66, 87, 50, 82, 33, 65, 83, 97, 49, 81,
 )
 
 
-def exchange_kernel(plan, tokens, out_grad, gate_pre, up_pre, hidden_grad, out_gate, out_up, out_down, *scratch):
+def exchange_kernel(plan, tokens, out_grad, gate_cot, up_cot, hidden, out_gate, out_up, out_down, *scratch):
     p = plan
     T, R, F, NB = p.tok, p.rows, p.hidden, p.n_batch
     n_flows = len(p.flows)
     scratch = list(scratch)
-    raw, hid, cot, tok_v, grad_v = (scratch.pop(0) for _ in range(5))
+    hid, cot, tok_v, grad_v = (scratch.pop(0) for _ in range(4))
     own = [scratch.pop(0) for _ in range(n_flows)]
     got = [scratch.pop(0) for _ in range(n_flows)]
-    raw_sem, cot_sem, load_g, swap_g, sent_g, load_t, swap_t, sent_t, send_x, recv_x, flow_send, flow_recv = scratch
+    cot_sem, grad_sem, tok_sem, swap_sent, flow_sent = (scratch.pop(0) for _ in range(5))
+    flow_got = scratch
     outs = (out_gate, out_up, out_down)
 
     b_me, s_me = lax.axis_index("batch"), lax.axis_index("seq")
@@ -449,69 +452,52 @@
 
     twin, across, crossed = device(0, 1), device(1 << X), device(1 << X, 1)
     peer = [device(1 << bit) for bit in range(4)]
-    sends = []
 
     def remote(src, dst, send_sem, recv_sem, to):
         return pltpu.make_async_remote_copy(
             src_ref=src, dst_ref=dst, send_sem=send_sem, recv_sem=recv_sem, device_id=to, device_id_type=MESH
         )
 
-    def start(copy):
-        copy.start()
-        sends.append(copy)
-
-    def raw_copies():
-        return [pltpu.make_async_copy(ref, raw.at[i, pl.ds(0, T)], raw_sem.at[0, i])
-                for i, ref in enumerate((gate_pre, up_pre, hidden_grad))]
-
-    def raw_swaps():
-        return [remote(ref, raw.at[i, pl.ds(T, T)], raw_sem.at[1, i], raw_sem.at[2, i], twin)
-                for i, ref in enumerate((gate_pre, up_pre, hidden_grad))]
+    def wait_bytes(ref, sem):
+        pltpu.make_async_copy(ref, ref, sem).wait()
 
     def grad_copy(u, m):
         return pltpu.make_async_copy(
-            out_grad.at[:, columns(u + 4 * m)], grad_v.at[u, m, pl.ds(0, T)], load_g.at[u, m])
+            out_grad.at[:, columns(u + 4 * m)], grad_v.at[u, m, pl.ds(0, T)], grad_sem.at[u, m])
 
     def grad_swap(u, m):
         return remote(out_grad.at[:, columns(u + 4 * m, 1)], grad_v.at[u, m, pl.ds(T, T)],
-                      sent_g.at[u, m], swap_g.at[u, m], twin)
+                      swap_sent.at[0], grad_sem.at[u, m], twin)
 
     def tok_copy(k, m):
         return pltpu.make_async_copy(
-            tokens.at[:, columns(2 * k + 4 * m)], tok_v.at[k, m, pl.ds(0, T)], load_t.at[k, m])
+            tokens.at[:, columns(2 * k + 4 * m)], tok_v.at[k, m, pl.ds(0, T)], tok_sem.at[k, m])
 
     def tok_swap(k, m):
         return remote(tokens.at[:, columns(2 * k + 4 * m, 1)], tok_v.at[k, m, pl.ds(T, T)],
-                      sent_t.at[k, m], swap_t.at[k, m], twin)
-
-    def tok_sends(k, m):
-        return [remote(tokens.at[:, columns(1 + 2 * k + 4 * m, c)], tok_v.at[k, m, pl.ds((2 + c) * T, T)],
-                       send_x.at[k, m, c], recv_x.at[k, m, c], to) for c, to in enumerate((across, crossed))]
-
-    def cot_send():
-        return remote(cot.at[pl.ds(0, T)], cot.at[pl.ds(2 * T, T)], cot_sem.at[0], cot_sem.at[1], across)
+                      swap_sent.at[1], tok_sem.at[k, m], twin)
+
+    def tok_send(k, m, c):
+        return remote(tokens.at[:, columns(1 + 2 * k + 4 * m, c)], tok_v.at[k, m, pl.ds((2 + c) * T, T)],
+                      swap_sent.at[2], tok_sem.at[k, m], crossed if c else across)
+
+    def cot_slot(slot):
+        return cot.at[pl.ds(slot * T, T)]
+
+    def cot_send(slot, to):
+        for i, ref in enumerate((gate_cot, up_cot)):
+            remote(ref, cot.at[pl.ds(slot * T, T), pl.ds(i * F, F)], cot_sem.at[0], cot_sem.at[slot], to).start()
 
     def cot_forward():
-        return remote(cot.at[pl.ds(2 * T, T)], cot.at[pl.ds(3 * T, T)], cot_sem.at[2], cot_sem.at[3], twin)
+        return remote(cot_slot(2), cot_slot(3), cot_sem.at[4], cot_sem.at[3], twin)
+
+    def hid_swap():
+        return remote(hidden, hid.at[pl.ds(T, T)], cot_sem.at[5], cot_sem.at[6], twin)
 
     def flow_copy(c, d):
         f = p.flows[c]
-        return remote(own[c].at[d], got[c].at[d], flow_send.at[c, d], flow_recv.at[c, d], peer[f.order[f.stage(d)]])
-
-    def activate(side):
-        step = 32
-        def body(i, carry):
-            at = pl.ds(pl.multiple_of(side * T + i * step, step), step)
-            gate_val = raw[0, at, :].astype(jnp.float32)
-            up_val = raw[1, at, :].astype(jnp.float32)
-            grad_val = raw[2, at, :].astype(jnp.float32)
-            sig = jax.nn.sigmoid(gate_val)
-            act = gate_val * sig
-            cot[at, 0:F] = (grad_val * up_val * sig * (1.0 + gate_val * (1.0 - sig))).astype(jnp.bfloat16)
-            cot[at, F:2 * F] = (grad_val * act).astype(jnp.bfloat16)
-            hid[at, :] = (act * up_val).astype(jnp.bfloat16)
-            return carry
-        lax.fori_loop(0, T // step, body, 0)
+        to = d - (1 << (f.n - 1 - f.stage(d)))
+        return remote(own[c].at[d], got[c].at[d], flow_sent.at[c], flow_got[c].at[to], peer[f.order[f.stage(d)]])
 
     dot = functools.partial(
         lax.dot_general, dimension_numbers=(((0,), (0,)), ((), ())), preferred_element_type=jnp.float32)
@@ -521,36 +507,36 @@
             if f.source == source:
                 own[c][f.dense(block)] = value[f.rows[0]:f.rows[1], f.cols[0]:f.cols[1]].astype(jnp.bfloat16)
 
+    waits = {"hid", "cot"}
+
     def down(u, m):
-        grad_copy(u, m).wait()
-        grad_swap(u, m).wait_recv()
+        if "hid" in waits:
+            waits.remove("hid")
+            hid_swap().wait_recv()
+        wait_bytes(grad_v.at[u, m], grad_sem.at[u, m])
         keep("down", u + 4 * m, dot(grad_v[u, m], hid[...]))
 
-    cot_left = [True]
-
     def up(k, m):
-        if cot_left:
-            cot_left.pop()
+        if "cot" in waits:
+            waits.remove("cot")
+            wait_bytes(cot_slot(1), cot_sem.at[1])
             cot_forward().wait_recv()
-        tok_copy(k, m).wait()
-        tok_swap(k, m).wait_recv()
-        for copy in tok_sends(k, m):
-            copy.wait_recv()
+        wait_bytes(tok_v.at[k, m], tok_sem.at[k, m])
         keep("up", 2 * k + 4 * m, dot(tok_v[k, m], cot[...]))
 
     def tok(k, m):
-        for copy in tok_sends(k, m):
-            start(copy)
+        for c in range(2):
+            tok_send(k, m, c).start()
 
     def forward():
-        cot_send().wait_recv()
-        start(cot_forward())
+        wait_bytes(cot_slot(2), cot_sem.at[2])
+        cot_forward().start()
 
     def advance(c, d):
         f = p.flows[c]
         entries = f.incoming(d)
-        for e in entries:
-            flow_copy(c, e).wait_recv()
+        if entries:
+            wait_bytes(own[c].at[pl.ds(0, len(entries))], flow_got[c].at[d])
         rows = f.shape[1]
         step = 32
 
@@ -568,15 +554,13 @@
         if entries:
             lax.fori_loop(0, rows // step, body, 0)
         if d:
-            start(flow_copy(c, d))
+            flow_copy(c, d).start()
 
     tasks = p.tasks()
     order = [tasks[i] for i in ORDER]
     downs = [t[1:] for t in order if t[0] == "down"]
     ups = [t[1:] for t in order if t[0] == "up"]
 
-    for copy in raw_copies():
-        copy.start()
     for u, m in downs:
         grad_copy(u, m).start()
     for k, m in ups:
@@ -588,53 +572,66 @@
         pl.semaphore_signal(barrier, inc=1, device_id=to, device_id_type=MESH)
     pl.semaphore_wait(barrier, len(peers))
 
-    for copy in raw_swaps():
-        start(copy)
+    cot_send(2, across)
+    hid_swap().start()
+    for u, m in downs[:4]:
+        grad_swap(u, m).start()
     tok(1, 3)
-    for u, m in downs:
-        start(grad_swap(u, m))
-    for copy in raw_copies():
-        copy.wait()
-    activate(0)
-    start(cot_send())
+    for u, m in downs[4:]:
+        grad_swap(u, m).start()
+    cot_send(1, twin)
     for k, m in ups:
-        start(tok_swap(k, m))
-    for copy in raw_swaps():
-        copy.wait_recv()
-    activate(1)
+        tok_swap(k, m).start()
+    hid[0:T] = hidden[...]
+    cot[0:T, 0:F] = gate_cot[...]
+    cot[0:T, F:2 * F] = up_cot[...]
 
     run = {"tok": tok, "forward": forward, "down": down, "up": up, "advance": advance}
     for task in order:
         run[task[0]](*task[1:])
 
-    for copy in sends:
-        copy.wait_send()
-
-
-def exchange_on_device(p, *args):
+    hid_swap().wait_send()
+    wait_bytes(cot.at[pl.ds(0, 2 * T)], cot_sem.at[0])
+    cot_forward().wait_send()
+    wait_bytes(grad_v.at[:, :, pl.ds(0, T)], swap_sent.at[0])
+    wait_bytes(tok_v.at[:, :, pl.ds(0, T)], swap_sent.at[1])
+    wait_bytes(tok_v.at[:, :, pl.ds(0, 2 * T)], swap_sent.at[2])
+    for c, f in enumerate(p.flows):
+        wait_bytes(own[c].at[pl.ds(1, f.shape[0] - 1)], flow_sent.at[c])
+
+
+def activate(gate_pre, up_pre, hidden_grad):
+    gate_val, up_val, grad_val = (a.astype(jnp.float32) for a in (gate_pre, up_pre, hidden_grad))
+    sig = jax.nn.sigmoid(gate_val)
+    act = gate_val * sig
+    gate_cot = grad_val * up_val * sig * (1.0 + gate_val * (1.0 - sig))
+    return tuple(a.astype(jnp.bfloat16) for a in (gate_cot, grad_val * act, act * up_val))
+
+
+def exchange_on_device(p, tokens, out_grad, gate_pre, up_pre, hidden_grad):
     T, R, F, bf16 = p.tok, p.rows, p.hidden, jnp.bfloat16
     scratch = [
-        pltpu.VMEM((3, 2 * T, F), bf16),
         pltpu.VMEM((2 * T, F), bf16),
         pltpu.VMEM((4 * T, 2 * F), bf16),
         pltpu.VMEM((2, 4, 4 * T, R), bf16),
         pltpu.VMEM((4, 4, 2 * T, R), bf16),
     ]
     scratch += [pltpu.VMEM(f.shape, bf16) for f in p.flows] * 2
-    dma, n_flows = pltpu.SemaphoreType.DMA, len(p.flows)
-    scratch += [dma((3, 3)), dma((4,))] + [dma((4, 4))] * 3 + [dma((2, 4))] * 3
-    scratch += [dma((2, 4, 2))] * 2 + [dma((n_flows, 16))] * 2
+    held = sum(2 * math.prod(ref.shape) for ref in scratch) + 4 * 3 * R * F + 2 * 3 * T * F
+    dma = pltpu.SemaphoreType.DMA
+    scratch += [dma((7,)), dma((4, 4)), dma((2, 4)), dma((3,)), dma((len(p.flows),))]
+    scratch += [dma((f.shape[0] // 2,)) for f in p.flows]
     out = jax.ShapeDtypeStruct((R, F), jnp.float32)
     return pl.pallas_call(
         functools.partial(exchange_kernel, p),
         out_shape=(out, out, out),
-        in_specs=[pl.BlockSpec(memory_space=pltpu.HBM)] * 5,
+        in_specs=[pl.BlockSpec(memory_space=pltpu.HBM)] * 2 + [pl.BlockSpec(memory_space=pltpu.VMEM)] * 3,
         out_specs=[pl.BlockSpec(memory_space=pltpu.VMEM)] * 3,
         scratch_shapes=scratch,
         compiler_params=pltpu.CompilerParams(
-            collective_id=0, has_side_effects=True, vmem_limit_bytes=67043328
+            collective_id=0, has_side_effects=True, vmem_limit_bytes=held + SPARE
         ),
-    )(*args)
+    )(tokens, out_grad, *activate(gate_pre, up_pre, hidden_grad))
 
 
 def on_device(n_batch, n_seq, tokens, out_grad, gate_pre, up_pre, hidden_grad):

time: 138 us -> 126 us (0.913)
  Pallas kernels: 131 us -> 121 us
  local copies, waits for them, and re-layouts: 6.19 us -> 2.64 us
  other arithmetic: 0 us -> 1.92 us
    pallas_call x1, Pallas kernels: 131 us -> 121 us  [exchange_on_device(): pl.pallas_call(functools.partial(exchange_kernel, p), out_shape=(out, out...]
    unnamed x3, local copies, waits for them, and re-layouts: 6.19 us -> 2.64 us
    convert_element_type x0 -> x1, other arithmetic: none -> 1.92 us  [activate(): a.astype(jnp.bfloat16)]
where the time goes in v2:
time: 126 us
  Pallas kernels  121 us (96%)
  local copies, waits for them, and re-layouts  2.64 us (2%)
  other arithmetic  1.92 us (2%)
    pallas_call x1, Pallas kernels, exchange_on_device(): pl.pallas_call(functools.partial(exchange_kernel, p), out_shape=(out, out...  121 us
    unnamed x3, local copies, waits for them, and re-layouts  2.64 us

profile of v2, /device:TPU:0, one launch (start us, length us, event | category | flops | bytes accessed | tf_op | source)
XLA Modules:
  0.0 125.7 jit_solution(1095733768831121345)
XLA Ops:
  0.6 1.9 %fusion.4 = (bf16[320,768]{1,0:T(8,128)(2,1)S(1)}, bf16[320,768]{1,0:T(8,128)(2,1)S(1)}, bf16[320,768]{1,0:T(8,128)(2,1)S(1)}) fusion(bf16[320,768]{1,0:T(8,128)(2,1)} %param.8, bf16[320,768]{1,0:T(8,128)(2,1)} %param.7, bf16[320,768]{1,0:T(8,128)(2,1)} %param.9), kind=kLoop, calls=%fused_computation.10 | loop fusion | flops 4423680 | bytes 2949120 | tf_op jit(solution)/shard_map/convert_element_type | solution.py:608
  2.6 120.5 %shard_map.76 = (f32[256,768]{1,0:T(8,128)S(1)}, f32[256,768]{1,0:T(8,128)S(1)}, f32[256,768]{1,0:T(8,128)S(1)}) custom-call(bf16[320,8192]{1,0:T(8,128)(2,1)} %tokens.1, bf16[320,8192]{1,0:T(8,128)(2,1)} %out_grad.1, bf16[320,768]{1,0:T(8,128)(2,1)S(1)} %get-tuple-element.4.gate_cot, bf16[320,768]{1,0:T(8,128)(2,1)S(1)} %get-tuple-element.5.up_cot, ...), custom_call_target="tpu_custom_call" | custom-call | tf_op jit(solution)/shard_map/pallas_call | solution.py:625
  123.1 0.9 copy.11
  124.0 0.9 copy.12
  124.8 0.9 copy.13

commit v3 on v2

--- a/solution.py
+++ b/solution.py
@@ -392,11 +392,16 @@
         unit, half = hidden // 6, R // 2
         full = (0, R)
         batch_first, y_first, x_first = (Z0, Z1, X, Y), (Y, X, Z0, Z1), (X, Y, Z0, Z1)
+        def up(a, b):
+            out = a // 6
+            return Flow("up", (Y, Z0, Z1), full, (a * unit, b * unit), out, out * hidden)
         def down(order, rows, a, b):
             return Flow("down", order, rows, (a * unit, b * unit), 2, 0)
         self.flows = [
-            Flow("up", (Y, Z0, Z1), full, (0, hidden), 0, 0),
-            Flow("up", (Y, Z0, Z1), full, (hidden, 2 * hidden), 1, hidden),
+            up(0, 3),
+            up(3, 6),
+            up(6, 9),
+            up(9, 12),
             down(batch_first, full, 0, 2),
             down(batch_first, (0, half), 2, 3),
             down(x_first, (half, R), 2, 3),
@@ -418,17 +423,18 @@
 
 SPARE = 6 << 20
 ORDER = (
-    22, 111, 60, 14, 15, 59, 24, 23, 19, 112, 13, 10, 16, 79, 20, 78,
-    12, 17, 57, 9, 21, 108, 11, 18, 74, 73, 80, 61, 71, 107, 70, 64,
-    109, 72, 76, 62, 53, 106, 8, 56, 105, 104, 58, 54, 110, 4, 32, 48,
-    75, 63, 2, 100, 40, 77, 28, 55, 1, 44, 69, 31, 6, 46, 36, 30,
-    5, 47, 27, 42, 3, 38, 26, 94, 102, 43, 39, 7, 29, 34, 89, 86,
-    96, 45, 92, 67, 90, 101, 25, 35, 103, 88, 37, 93, 98, 68, 91, 95,
-    52, 41, 51, 84, 99, 85, 66, 87, 50, 82, 33, 65, 83, 97, 49, 81,
+    24, 128, 96, 80, 16, 10, 21, 23, 22, 76, 13, 17, 126, 12, 18, 9,
+    20, 72, 19, 123, 78, 77, 74, 88, 121, 127, 122, 14, 15, 70, 93, 79,
+    92, 8, 11, 89, 125, 124, 69, 75, 120, 4, 32, 91, 48, 94, 95, 73,
+    2, 116, 118, 40, 90, 56, 71, 28, 64, 86, 44, 6, 87, 31, 36, 1,
+    46, 119, 85, 52, 114, 38, 54, 27, 42, 62, 60, 112, 5, 34, 30, 55,
+    47, 63, 39, 3, 115, 50, 104, 117, 26, 43, 29, 110, 53, 7, 45, 35,
+    58, 102, 107, 51, 108, 84, 37, 111, 68, 25, 106, 61, 67, 103, 109, 100,
+    66, 82, 59, 33, 83, 98, 41, 101, 105, 99, 113, 49, 65, 81, 57, 97,
 )
 
 
-def exchange_kernel(plan, tokens, out_grad, gate_cot, up_cot, hidden, out_gate, out_up, out_down, *scratch):
+def exchange_kernel(plan, tokens, out_grad, gate_cot, up_cot, hidden, out, *scratch):
     p = plan
     T, R, F, NB = p.tok, p.rows, p.hidden, p.n_batch
     n_flows = len(p.flows)
@@ -438,10 +444,9 @@
     got = [scratch.pop(0) for _ in range(n_flows)]
     cot_sem, grad_sem, tok_sem, swap_sent, flow_sent = (scratch.pop(0) for _ in range(5))
     flow_got = scratch
-    outs = (out_gate, out_up, out_down)
+    outs = [out.at[:, pl.ds(i * F, F)] for i in range(3)]
 
     b_me, s_me = lax.axis_index("batch"), lax.axis_index("seq")
-    core, chip = s_me % 2, s_me // 2
 
     def device(block, other=0):
         return (flip(b_me, block >> 2), flip(s_me, 2 * (block & 3) + other))
@@ -621,17 +626,17 @@
     dma = pltpu.SemaphoreType.DMA
     scratch += [dma((7,)), dma((4, 4)), dma((2, 4)), dma((3,)), dma((len(p.flows),))]
     scratch += [dma((f.shape[0] // 2,)) for f in p.flows]
-    out = jax.ShapeDtypeStruct((R, F), jnp.float32)
-    return pl.pallas_call(
+    out = pl.pallas_call(
         functools.partial(exchange_kernel, p),
-        out_shape=(out, out, out),
+        out_shape=jax.ShapeDtypeStruct((R, 3 * F), jnp.float32),
         in_specs=[pl.BlockSpec(memory_space=pltpu.HBM)] * 2 + [pl.BlockSpec(memory_space=pltpu.VMEM)] * 3,
-        out_specs=[pl.BlockSpec(memory_space=pltpu.VMEM)] * 3,
+        out_specs=pl.BlockSpec(memory_space=pltpu.VMEM),
         scratch_shapes=scratch,
         compiler_params=pltpu.CompilerParams(
             collective_id=0, has_side_effects=True, vmem_limit_bytes=held + SPARE
         ),
     )(tokens, out_grad, *activate(gate_pre, up_pre, hidden_grad))
+    return out[:, :F], out[:, F:2 * F], out[:, 2 * F:]
 
 
 def on_device(n_batch, n_seq, tokens, out_grad, gate_pre, up_pre, hidden_grad):

time: 126 us -> 122 us (0.968)
  Pallas kernels: 121 us -> 118 us
    unnamed x3 -> x0, local copies, waits for them, and re-layouts: 2.64 us -> none
    pallas_call x1, Pallas kernels: 121 us -> 118 us  [exchange_on_device(): pl.pallas_call(functools.partial(exchange_kernel, p), out_shape=jax.Shape...]
    slice x0 -> x1, local copies, waits for them, and re-layouts: none -> 1.45 us  [exchange_on_device(): return (out[:, :F], out[:, F:2 * F], out[:, 2 * F:])]
where the time goes in v3:
time: 122 us
  Pallas kernels  118 us (97%)
  other arithmetic  1.92 us (2%)
  local copies, waits for them, and re-layouts  1.45 us (1%)
    pallas_call x1, Pallas kernels, exchange_on_device(): pl.pallas_call(functools.partial(exchange_kernel, p), out_shape=jax.Shape...  118 us

profile of v3, /device:TPU:0, one launch (start us, length us, event | category | flops | bytes accessed | tf_op | source)
XLA Modules:
  0.0 122.1 jit_solution(1412126719848288222)
XLA Ops:
  0.6 1.9 %fusion.4 = (bf16[320,768]{1,0:T(8,128)(2,1)S(1)}, bf16[320,768]{1,0:T(8,128)(2,1)S(1)}, bf16[320,768]{1,0:T(8,128)(2,1)S(1)}) fusion(bf16[320,768]{1,0:T(8,128)(2,1)} %param.8, bf16[320,768]{1,0:T(8,128)(2,1)} %param.7, bf16[320,768]{1,0:T(8,128)(2,1)} %param.9), kind=kLoop, calls=%fused_computation.10 | loop fusion | flops 4423680 | bytes 2949120 | tf_op jit(solution)/shard_map/convert_element_type | solution.py:613
  2.6 118.1 %shard_map.76 = f32[256,2304]{1,0:T(8,128)S(1)} custom-call(bf16[320,8192]{1,0:T(8,128)(2,1)} %tokens.1, bf16[320,8192]{1,0:T(8,128)(2,1)} %out_grad.1, bf16[320,768]{1,0:T(8,128)(2,1)S(1)} %get-tuple-element.7.gate_cot, bf16[320,768]{1,0:T(8,128)(2,1)S(1)} %get-tuple-element.8.up_cot, bf16[320,768]{1,0:T(8,128)(2,1)S(1)} %get-tuple-element.6.hidden), custom_call_target="tpu_custom_call" | custom-call | tf_op jit(solution)/shard_map/pallas_call | solution.py:629
  120.6 1.4 %fusion.9 = (f32[256,768]{1,0:T(8,128)}, f32[256,768]{1,0:T(8,128)}, f32[256,768]{1,0:T(8,128)}) fusion(f32[256,2304]{1,0:T(8,128)S(1)} %shard_map.76), kind=kLoop, calls=%fused_computation.15 | loop fusion | bytes 4718592 | tf_op jit(solution)/shard_map/slice | solution.py:639

commit v4 on v3

--- a/solution.py
+++ b/solution.py
@@ -423,14 +423,14 @@
 
 SPARE = 6 << 20
 ORDER = (
-    24, 128, 96, 80, 16, 10, 21, 23, 22, 76, 13, 17, 126, 12, 18, 9,
-    20, 72, 19, 123, 78, 77, 74, 88, 121, 127, 122, 14, 15, 70, 93, 79,
-    92, 8, 11, 89, 125, 124, 69, 75, 120, 4, 32, 91, 48, 94, 95, 73,
-    2, 116, 118, 40, 90, 56, 71, 28, 64, 86, 44, 6, 87, 31, 36, 1,
-    46, 119, 85, 52, 114, 38, 54, 27, 42, 62, 60, 112, 5, 34, 30, 55,
-    47, 63, 39, 3, 115, 50, 104, 117, 26, 43, 29, 110, 53, 7, 45, 35,
-    58, 102, 107, 51, 108, 84, 37, 111, 68, 25, 106, 61, 67, 103, 109, 100,
-    66, 82, 59, 33, 83, 98, 41, 101, 105, 99, 113, 49, 65, 81, 57, 97,
+    20, 124, 78, 19, 24, 22, 23, 127, 122, 12, 80, 17, 70, 11, 77, 16,
+    21, 128, 79, 69, 14, 121, 93, 75, 85, 18, 10, 92, 72, 15, 123, 96,
+    74, 8, 71, 4, 94, 6, 126, 76, 125, 89, 95, 32, 56, 2, 90, 48,
+    112, 73, 28, 91, 52, 86, 40, 88, 9, 120, 44, 64, 31, 36, 46, 27,
+    1, 116, 119, 60, 87, 38, 5, 110, 54, 42, 34, 30, 111, 55, 104, 13,
+    118, 3, 47, 39, 62, 50, 108, 115, 63, 26, 51, 114, 58, 109, 84, 103,
+    29, 7, 102, 53, 35, 43, 45, 106, 68, 117, 100, 37, 105, 66, 59, 107,
+    67, 61, 25, 33, 113, 82, 99, 83, 49, 98, 101, 65, 41, 57, 81, 97,
 )
 
 
@@ -566,15 +566,17 @@
     downs = [t[1:] for t in order if t[0] == "down"]
     ups = [t[1:] for t in order if t[0] == "up"]
 
+    barrier = pltpu.get_barrier_semaphore()
+    peers = [twin, crossed] + peer
+    for to in peers[::-1]:
+        pl.semaphore_signal(barrier, inc=1, device_id=to, device_id_type=MESH)
     for u, m in downs:
         grad_copy(u, m).start()
     for k, m in ups:
         tok_copy(k, m).start()
-
-    barrier = pltpu.get_barrier_semaphore()
-    peers = [twin, crossed] + peer
-    for to in peers:
-        pl.semaphore_signal(barrier, inc=1, device_id=to, device_id_type=MESH)
+    hid[0:T] = hidden[...]
+    cot[0:T, 0:F] = gate_cot[...]
+    cot[0:T, F:2 * F] = up_cot[...]
     pl.semaphore_wait(barrier, len(peers))
 
     cot_send(2, across)
@@ -587,9 +589,6 @@
     cot_send(1, twin)
     for k, m in ups:
         tok_swap(k, m).start()
-    hid[0:T] = hidden[...]
-    cot[0:T, 0:F] = gate_cot[...]
-    cot[0:T, F:2 * F] = up_cot[...]
 
     run = {"tok": tok, "forward": forward, "down": down, "up": up, "advance": advance}
     for task in order:

time: 122 us -> 122 us (level)
  no operation moved by 1% of the time
where the time goes in v4:
time: 122 us
  Pallas kernels  118 us (97%)
  other arithmetic  1.92 us (2%)
  local copies, waits for them, and re-layouts  1.45 us (1%)
    pallas_call x1, Pallas kernels, exchange_on_device(): pl.pallas_call(functools.partial(exchange_kernel, p), out_shape=jax.Shape...  118 us

profile of v4, /device:TPU:0, one launch (start us, length us, event | category | flops | bytes accessed | tf_op | source)
XLA Modules:
  0.0 121.6 jit_solution(5778777996641790012)
XLA Ops:
  0.6 1.9 %fusion.4 = (bf16[320,768]{1,0:T(8,128)(2,1)S(1)}, bf16[320,768]{1,0:T(8,128)(2,1)S(1)}, bf16[320,768]{1,0:T(8,128)(2,1)S(1)}) fusion(bf16[320,768]{1,0:T(8,128)(2,1)} %param.8, bf16[320,768]{1,0:T(8,128)(2,1)} %param.7, bf16[320,768]{1,0:T(8,128)(2,1)} %param.9), kind=kLoop, calls=%fused_computation.10 | loop fusion | flops 4423680 | bytes 2949120 | tf_op jit(solution)/shard_map/convert_element_type | solution.py:612
  2.6 117.5 %shard_map.76 = f32[256,2304]{1,0:T(8,128)S(1)} custom-call(bf16[320,8192]{1,0:T(8,128)(2,1)} %tokens.1, bf16[320,8192]{1,0:T(8,128)(2,1)} %out_grad.1, bf16[320,768]{1,0:T(8,128)(2,1)S(1)} %get-tuple-element.7.gate_cot, bf16[320,768]{1,0:T(8,128)(2,1)S(1)} %get-tuple-element.8.up_cot, bf16[320,768]{1,0:T(8,128)(2,1)S(1)} %get-tuple-element.6.hidden), custom_call_target="tpu_custom_call" | custom-call | tf_op jit(solution)/shard_map/pallas_call | solution.py:628
  120.1 1.4 %fusion.9 = (f32[256,768]{1,0:T(8,128)}, f32[256,768]{1,0:T(8,128)}, f32[256,768]{1,0:T(8,128)}) fusion(f32[256,2304]{1,0:T(8,128)S(1)} %shard_map.76), kind=kLoop, calls=%fused_computation.15 | loop fusion | bytes 4718592 | tf_op jit(solution)/shard_map/slice | solution.py:638
